TPU v7x, 32 devices: a whole 2x2x4 slice. The times are simulated.
32 devices in a mesh: batch: 4 (over x, core), lat: 8 (over z, y).
Axes of the slice: x: 2, y: 2, z: 4, core: 2. Of those that a mesh axis runs over, the one named last changes fastest.
Arguments:
- predicted: bfloat16 [4, 73, 192, 1440], P('batch', None, 'lat'), may hold values from -64 to 64
- target: bfloat16 [4, 73, 192, 1440], P('batch', None, 'lat'), may hold values from -128 to 128
- legendre_basis: bfloat16 [192, 96, 720], P(None, ('batch', 'lat')), may hold values from -1 to 1
Outputs:
- spectra: float32 [2, 73, 720], replicated
- channel_loss: float32 [73], replicated
All inputs are finite; a program needn't handle non-finite values.
Results may differ from a plain program's by a relative error of at most 0.0003.
Values may be sent and summed in bfloat16 or wider, within the bound.
No kernel may reach another device: no remote copies, remote signals or barrier semaphores. Data moves between devices by JAX's collectives and lax.ppermute only.
A program may use at most 128 MiB of HBM per device.

v0:
```python
import math
import jax
import jax.numpy as jnp
from jax import lax
from jax.sharding import PartitionSpec as P


def fourier_table(lon_count, order_count):
    lon_ids = jnp.arange(lon_count, dtype=jnp.int32)
    order_ids = jnp.arange(order_count, dtype=jnp.int32)
    product_ids = lon_ids[:, None] * order_ids[None, :] % lon_count
    angles = 2.0 * math.pi / lon_count * product_ids.astype(jnp.float32)
    inv_root = 1.0 / math.sqrt(lon_count)
    return jnp.stack([jnp.cos(angles) * inv_root, -jnp.sin(angles) * inv_root], axis=1).astype(
        jnp.bfloat16
    )


def band_energy(fourier, basis_block, orders):
    coefficients = jnp.einsum(
        "fpmbcn,nml->fpmbcl", fourier, basis_block, preferred_element_type=jnp.float32
    )
    squares = jnp.sum(coefficients * coefficients, axis=1)
    weights = jnp.where(orders == 0, 1.0, 2.0).astype(jnp.float32)
    return jnp.sum(squares * weights[None, :, None, None, None], axis=(1, 2))


def body(predicted, target, legendre_basis):
    groups = lax.axis_size("batch")
    band_count = lax.axis_size("lat")
    per_dev = legendre_basis.shape[1]
    order_count = per_dev * groups * band_count
    dft_table = fourier_table(predicted.shape[3], order_count)
    band_id = lax.axis_index("lat")

    def transform(field_in):
        return jnp.einsum(
            "bcnk,kpm->pmbcn", field_in, dft_table, preferred_element_type=jnp.float32
        ).astype(jnp.bfloat16)

    fourier = jnp.stack([transform(predicted), transform(target)], axis=0)
    members = fourier.shape[3]
    channels = fourier.shape[4]
    lat_rows = fourier.shape[5]
    fourier = fourier.reshape(2, 2, groups, band_count, per_dev, members, channels, lat_rows)
    arrived = lax.all_to_all(fourier, "lat", split_axis=3, concat_axis=7, tiled=True)
    arrived = arrived.reshape(
        2, 2, groups * per_dev, arrived.shape[5], arrived.shape[6], arrived.shape[7]
    )
    basis_block = lax.all_gather(legendre_basis, "batch", axis=1, tiled=True)
    taken = basis_block.shape[1]
    gathered_ids = jnp.arange(taken, dtype=jnp.int32)
    orders = (
        gathered_ids // per_dev * band_count * per_dev + band_id * per_dev + gathered_ids % per_dev
    )
    partial_value = band_energy(arrived, basis_block, orders)
    energy = lax.psum(partial_value, "lat")
    energy = lax.psum(energy, "batch")
    spectra = energy / (predicted.shape[0] * groups * order_count)
    log_spectra = jnp.log(spectra + 1e-06)
    channel_loss = jnp.mean((log_spectra[0] - log_spectra[1]) ** 2, axis=1)
    return (spectra, channel_loss)


def solution(mesh):
    placed = (
        P("batch", None, "lat", None),
        P("batch", None, "lat", None),
        P(None, ("batch", "lat"), None),
    )
    return jax.shard_map(body, mesh=mesh, in_specs=placed, out_specs=(P(), P()), check_vma=False)
```

profile of v0, /device:TPU:0, one launch (start us, length us, event | category | flops | bytes accessed | tf_op | source)
XLA Modules:
  0.0 212.2 jit_solution(11625327290755649896)
XLA Ops:
  7.2 0.0 all-gather.2.cloned.1.call-start
  7.2 0.7 all-gather.2.cloned.1.call-update
  7.9 2.6 %multiply_convert_fusion = (bf16[1440,1,96]{0,2,1:T(8,128)(2,1)S(1)}, bf16[1440,1,96]{0,2,1:T(8,128)(2,1)S(1)}) fusion(), kind=kLoop, calls=%fused_computation.17 | loop fusion | flops 1935360 | bytes 552960 | tf_op jit(solution)/shard_map/convert.1
  10.5 0.0 copy-start
  10.5 0.0 copy-start.1
  10.5 0.7 copy-done
  11.2 0.1 copy-done.1
  11.3 4.8 %fusion.8 = bf16[2,96,73,24]{1,2,3,0:T(8,128)(2,1)S(1)} fusion(bf16[73,24,1440]{2,1,0:T(8,128)(2,1)} %bitcast.33, bf16[1440,1,96]{0,2,1:T(8,128)(2,1)S(1)} %get-tuple-element.4, bf16[1440,1,96]{0,2,1:T(8,128)(2,1)S(1)} %get-tuple-element.5), kind=kOutput, calls=%fused_computation.11 | convolution fusion | flops 970228224 | bytes 6271488 | tf_op jit(solution)/shard_map/bcnk,kpm->pmbcn/dot_general | solution.py:37
  16.1 0.9 copy.29
  17.0 5.5 %fusion.11 = bf16[2,96,73,24]{1,2,3,0:T(8,128)(2,1)S(1)} fusion(bf16[73,24,1440]{2,1,0:T(8,128)(2,1)} %bitcast.34, bf16[1440,1,96]{0,2,1:T(8,128)(2,1)} %copy-done, bf16[1440,1,96]{0,2,1:T(8,128)(2,1)} %copy-done.1), kind=kOutput, calls=%fused_computation.12 | convolution fusion | flops 970228224 | bytes 6271488 | tf_op jit(solution)/shard_map/bcnk,kpm->pmbcn/dot_general | solution.py:37
  22.5 0.9 copy.31
  23.3 0.5 pad_maximum_fusion
  23.9 2.0 copy.32
  25.9 7.5 %all-to-all-start = ((bf16[2,2,4,8,3,1,73,24]{6,7,4,2,1,5,0,3:T(8,128)(2,1)}), bf16[2,2,4,8,3,1,73,24]{6,7,4,2,1,5,0,3:T(8,128)(2,1)S(1)}, u32[]{:S(2)}, u32[]{:S(2)}) async-start(bf16[2,2,4,8,3,1,73,24]{6,7,4,2,1,5,0,3:T(8,128)(2,1)} %copy.32), calls=%async_computation | async-start | bytes 4718592 | tf_op jit(solution)/shard_map/all_to_all | solution.py:46
  33.5 0.0 all-reduce.3.cloned.1.call-start
  33.5 53.6 %all-to-all-done = bf16[2,2,4,8,3,1,73,24]{6,7,4,2,1,5,0,3:T(8,128)(2,1)S(1)} async-done(((bf16[2,2,4,8,3,1,73,24]{6,7,4,2,1,5,0,3:T(8,128)(2,1)}), bf16[2,2,4,8,3,1,73,24]{6,7,4,2,1,5,0,3:T(8,128)(2,1)S(1)}, u32[]{:S(2)}, u32[]{:S(2)}) %all-to-all-start) | async-done | bytes 1345568 | tf_op jit(solution)/shard_map/all_to_all | solution.py:46
  87.1 2.1 copy.33
  89.2 0.0 all-gather.2.cloned.1.call-done
  89.2 5.1 %multiply_reduce_fusion = f32[12,2,73,720]{3,2,1,0:T(8,128)S(1)} fusion(bf16[192,12,720]{2,0,1:T(8,128)(2,1)} %all-gather.2.cloned.1.call-done, bf16[2,2,12,73,192]{3,4,2,1,0:T(8,128)(2,1)} %bitcast.30), kind=kOutput, calls=%fused_computation | convolution fusion | flops 972570240 | bytes 9709056 | tf_op jit(solution)/shard_map/fpmbcn,nml->fpmbcl/dot_general | solution.py:20
  94.3 0.6 multiply_reduce_fusion.1
  94.9 1.1 copy.40
  96.0 0.0 all-reduce.3.cloned.1.call-update
  96.1 0.0 all-reduce.5.cloned.1.call-start
  96.1 71.4 %all-reduce.3.cloned.1.call-done = f32[2,73,720]{2,0,1:T(2,128)} async-done(((f32[2,73,720]{2,0,1:T(2,128)}), f32[2,73,720]{2,0,1:T(2,128)}) %all-reduce.3.cloned.1.call-update) | async-done | bytes 420496 | tf_op jit(solution)/shard_map/psum | solution.py:57
  167.5 0.0 all-reduce.5.cloned.1.call-update
  167.6 34.7 %all-reduce.5.cloned.1.call-done = f32[2,73,720]{2,0,1:T(2,128)} async-done(((f32[2,73,720]{2,0,1:T(2,128)}), f32[2,73,720]{2,0,1:T(2,128)}) %all-reduce.5.cloned.1.call-update) | async-done | bytes 420496 | tf_op jit(solution)/shard_map/psum | solution.py:58
  202.2 2.2 %add_log_fusion = (f32[2,73,720]{2,0,1:T(2,128)S(1)}, f32[2,73,720]{2,0,1:T(2,128)}) fusion(f32[2,73,720]{2,0,1:T(2,128)} %all-reduce.5.cloned.1.call-done), kind=kLoop, calls=%fused_computation.23 | loop fusion | flops 210240 | bytes 1261440 | tf_op jit(solution)/shard_map/log | solution.py:60
  204.5 0.6 fusion.20
  205.1 0.5 broadcast_multiply_fusion.1
  (1 shorter events, 0.0 us)
Async XLA Ops:
  7.2 82.1 %all-gather.2.cloned.1.call-start = ((), (), s32[]{:S(2)}) async-start(), calls=%async_computation.1 | async-start | bytes 4423680 | tf_op jit(solution)/shard_map/all_gather | solution.py:50
  10.5 0.7 copy-start
  10.5 0.8 copy-start.1
  25.9 61.2 %all-to-all-start = ((bf16[2,2,4,8,3,1,73,24]{6,7,4,2,1,5,0,3:T(8,128)(2,1)}), bf16[2,2,4,8,3,1,73,24]{6,7,4,2,1,5,0,3:T(8,128)(2,1)S(1)}, u32[]{:S(2)}, u32[]{:S(2)}) async-start(bf16[2,2,4,8,3,1,73,24]{6,7,4,2,1,5,0,3:T(8,128)(2,1)} %copy.32), calls=%async_computation | async-start | bytes 4718592 | tf_op jit(solution)/shard_map/all_to_all | solution.py:46
  33.5 134.1 %all-reduce.3.cloned.1.call-start = ((), (), s32[]{:S(2)}) async-start(), calls=%async_computation.2 | async-start | bytes 897024 | tf_op jit(solution)/shard_map/psum | solution.py:57
  96.1 106.2 %all-reduce.5.cloned.1.call-start = ((), (), s32[]{:S(2)}) async-start(), calls=%async_computation.3 | async-start | bytes 897024 | tf_op jit(solution)/shard_map/psum | solution.py:58
Sparse Core Ops, SparseCore 0:
  9.5 33.4 all-gather.1
  96.2 71.2 all-reduce.2
  169.9 32.2 all-reduce.4
where the time goes:
time: 212 us
  waiting for transfers between devices  160 us (75%)
  matrix products  15.4 us (7%)
  between operations  13.8 us (7%)
  local copies, waits for them, and re-layouts  7.77 us (4%)
  starting transfers between devices  7.66 us (4%)
  other arithmetic  7.07 us (3%)
    psum x1, waiting for transfers between devices, body(): energy = lax.psum(partial_value, 'lat')  71.4 us
    all_to_all x1, waiting for transfers between devices, body(): lax.all_to_all(fourier, 'lat', split_axis=3, concat_axis=7, tiled=True)  53.6 us
    psum x1, waiting for transfers between devices, body(): energy = lax.psum(energy, 'batch')  34.7 us
    dot_general x2, matrix products, transform(): jnp.einsum('bcnk,kpm->pmbcn', field_in, dft_table, preferred_element_type...  10.3 us
    all_to_all x1, starting transfers between devices, body(): lax.all_to_all(fourier, 'lat', split_axis=3, concat_axis=7, tiled=True)  7.55 us
    dot_general x1, matrix products, band_energy(): jnp.einsum('fpmbcn,nml->fpmbcl', fourier, basis_block, preferred_element_...  5.1 us
  transfers between devices with their start and end apart: 4, of which 3 were waited for; matrix products, arithmetic and copies ran while one was open for 9% of the time, Pallas kernels for 0%

commit v1 on v0

--- a/solution.py
+++ b/solution.py
@@ -55,7 +55,7 @@
     )
     partial_value = band_energy(arrived, basis_block, orders)
     energy = lax.psum(partial_value, "lat")
-    energy = lax.psum(energy, "batch")
+    energy = jnp.sum(lax.all_gather(energy, "batch"), axis=0)
     spectra = energy / (predicted.shape[0] * groups * order_count)
     log_spectra = jnp.log(spectra + 1e-06)
     channel_loss = jnp.mean((log_spectra[0] - log_spectra[1]) ** 2, axis=1)

time: 212 us -> 201 us (0.948)
  waiting for transfers between devices: 160 us -> 148 us
    psum x1 -> x0, waiting for transfers between devices: 34.7 us -> none  [body(): energy = lax.psum(energy, 'batch')]
    all_gather x0 -> x1, waiting for transfers between devices: none -> 21.8 us  [body(): energy = jnp.sum(lax.all_gather(energy, 'batch'), axis=0)]
    reduce_sum x0 -> x1, other arithmetic: none -> 2.36 us  [body(): energy = jnp.sum(lax.all_gather(energy, 'batch'), axis=0)]
  transfers between devices with their start and end apart: 4 -> 4, of which waited for: 3 -> 3; matrix products, arithmetic and copies ran while one was open for 9% -> 10% of each run, Pallas kernels for 0% -> 0%
where the time goes in v1:
time: 201 us
  waiting for transfers between devices  148 us (74%)
  matrix products  15.4 us (8%)
  between operations  13.8 us (7%)
  other arithmetic  8.42 us (4%)
  local copies, waits for them, and re-layouts  7.77 us (4%)
  starting transfers between devices  7.66 us (4%)
    psum x1, waiting for transfers between devices, body(): energy = lax.psum(partial_value, 'lat')  71.4 us
    all_to_all x1, waiting for transfers between devices, body(): lax.all_to_all(fourier, 'lat', split_axis=3, concat_axis=7, tiled=True)  53.6 us
    all_gather x1, waiting for transfers between devices, body(): energy = jnp.sum(lax.all_gather(energy, 'batch'), axis=0)  21.8 us
    dot_general x2, matrix products, transform(): jnp.einsum('bcnk,kpm->pmbcn', field_in, dft_table, preferred_element_type...  10.3 us
    all_to_all x1, starting transfers between devices, body(): lax.all_to_all(fourier, 'lat', split_axis=3, concat_axis=7, tiled=True)  7.55 us
    dot_general x1, matrix products, band_energy(): jnp.einsum('fpmbcn,nml->fpmbcl', fourier, basis_block, preferred_element_...  5.1 us
  transfers between devices with their start and end apart: 4, of which 3 were waited for; matrix products, arithmetic and copies ran while one was open for 10% of the time, Pallas kernels for 0%

profile of v1, /device:TPU:0, one launch (start us, length us, event | category | flops | bytes accessed | tf_op | source)
XLA Modules:
  0.0 200.7 jit_solution(17926567921007779769)
XLA Ops:
  7.2 0.0 all-gather.3.cloned.1.call-start
  7.2 0.7 all-gather.3.cloned.1.call-update
  7.9 2.6 %multiply_convert_fusion = (bf16[1440,1,96]{0,2,1:T(8,128)(2,1)S(1)}, bf16[1440,1,96]{0,2,1:T(8,128)(2,1)S(1)}) fusion(), kind=kLoop, calls=%fused_computation.17 | loop fusion | flops 1935360 | bytes 552960 | tf_op jit(solution)/shard_map/convert.1
  10.5 0.0 copy-start
  10.5 0.0 copy-start.1
  10.5 0.7 copy-done
  11.2 0.1 copy-done.1
  11.3 4.8 %fusion.8 = bf16[2,96,73,24]{1,2,3,0:T(8,128)(2,1)S(1)} fusion(bf16[73,24,1440]{2,1,0:T(8,128)(2,1)} %bitcast.37, bf16[1440,1,96]{0,2,1:T(8,128)(2,1)S(1)} %get-tuple-element.4, bf16[1440,1,96]{0,2,1:T(8,128)(2,1)S(1)} %get-tuple-element.5), kind=kOutput, calls=%fused_computation.11 | convolution fusion | flops 970228224 | bytes 6271488 | tf_op jit(solution)/shard_map/bcnk,kpm->pmbcn/dot_general | solution.py:37
  16.1 0.9 copy.29
  17.0 5.5 %fusion.11 = bf16[2,96,73,24]{1,2,3,0:T(8,128)(2,1)S(1)} fusion(bf16[73,24,1440]{2,1,0:T(8,128)(2,1)} %bitcast.38, bf16[1440,1,96]{0,2,1:T(8,128)(2,1)} %copy-done, bf16[1440,1,96]{0,2,1:T(8,128)(2,1)} %copy-done.1), kind=kOutput, calls=%fused_computation.12 | convolution fusion | flops 970228224 | bytes 6271488 | tf_op jit(solution)/shard_map/bcnk,kpm->pmbcn/dot_general | solution.py:37
  22.5 0.9 copy.31
  23.3 0.5 pad_maximum_fusion
  23.9 2.0 %copy.32 = bf16[2,2,4,8,3,1,73,24]{6,7,4,2,1,5,0,3:T(8,128)(2,1)} copy(bf16[2,2,4,8,3,1,73,24]{6,7,4,3,2,1,5,0:T(8,128)(2,1)S(1)} %pad_maximum_fusion) | data formatting | bytes 2691072 | tf_op jit(solution)/shard_map/stack | solution.py:41
  25.9 7.5 %all-to-all-start = ((bf16[2,2,4,8,3,1,73,24]{6,7,4,2,1,5,0,3:T(8,128)(2,1)}), bf16[2,2,4,8,3,1,73,24]{6,7,4,2,1,5,0,3:T(8,128)(2,1)S(1)}, u32[]{:S(2)}, u32[]{:S(2)}) async-start(bf16[2,2,4,8,3,1,73,24]{6,7,4,2,1,5,0,3:T(8,128)(2,1)} %copy.32), calls=%async_computation | async-start | bytes 4718592 | tf_op jit(solution)/shard_map/all_to_all | solution.py:46
  33.5 0.0 all-reduce.2.cloned.1.call-start
  33.5 53.6 %all-to-all-done = bf16[2,2,4,8,3,1,73,24]{6,7,4,2,1,5,0,3:T(8,128)(2,1)S(1)} async-done(((bf16[2,2,4,8,3,1,73,24]{6,7,4,2,1,5,0,3:T(8,128)(2,1)}), bf16[2,2,4,8,3,1,73,24]{6,7,4,2,1,5,0,3:T(8,128)(2,1)S(1)}, u32[]{:S(2)}, u32[]{:S(2)}) %all-to-all-start) | async-done | bytes 1345568 | tf_op jit(solution)/shard_map/all_to_all | solution.py:46
  87.1 2.1 %copy.33 = bf16[2,2,4,1,3,1,73,8,24]{6,8,7,4,2,1,0,5,3:T(8,128)(2,1)} copy(bf16[2,2,4,1,3,1,73,8,24]{6,8,4,2,1,0,7,5,3:T(8,128)(2,1)S(1)} %bitcast.32) | data formatting | bytes 2691072 | tf_op jit(solution)/shard_map/all_to_all | solution.py:46
  89.2 0.0 all-gather.3.cloned.1.call-done
  89.2 5.1 %multiply_reduce_fusion = f32[12,2,73,720]{3,2,1,0:T(8,128)S(1)} fusion(bf16[192,12,720]{2,0,1:T(8,128)(2,1)} %all-gather.3.cloned.1.call-done, bf16[2,2,12,73,192]{3,4,2,1,0:T(8,128)(2,1)} %bitcast.33), kind=kOutput, calls=%fused_computation | convolution fusion | flops 972570240 | bytes 9709056 | tf_op jit(solution)/shard_map/fpmbcn,nml->fpmbcl/dot_general | solution.py:20
  94.3 0.6 multiply_reduce_fusion.1
  94.9 1.1 copy.56
  96.0 0.0 all-reduce.2.cloned.1.call-update
  96.1 0.0 all-gather.5.cloned.1.call-start
  96.1 71.4 %all-reduce.2.cloned.1.call-done = f32[1,2,73,720]{3,1,2,0:T(2,128)} async-done(((f32[1,2,73,720]{3,1,2,0:T(2,128)}), f32[1,2,73,720]{3,1,2,0:T(2,128)}) %all-reduce.2.cloned.1.call-update) | async-done | bytes 420496 | tf_op jit(solution)/shard_map/psum | solution.py:57
  167.5 0.0 all-gather.5.cloned.1.call-update
  167.6 21.8 %all-gather.5.cloned.1.call-done = f32[4,2,73,720]{3,1,2,0:T(2,128)} async-done(((f32[1,2,73,720]{3,1,2,0:T(2,128)}), f32[4,2,73,720]{3,1,2,0:T(2,128)}) %all-gather.5.cloned.1.call-update) | async-done | bytes 1681936 | tf_op jit(solution)/shard_map/all_gather | solution.py:58
  189.4 2.4 %reduce_sum.38 = f32[2,73,720]{2,0,1:T(2,128)S(1)} reduce(f32[4,2,73,720]{3,1,2,0:T(2,128)} %all-gather.5.cloned.1.call-done, f32[]{:T(128)} %constant.47.clone.1), dimensions={0}, to_apply=%region_3.4 | reduce | flops 315360 | bytes 2102404 | tf_op jit(solution)/shard_map/reduce_sum | solution.py:58
  191.8 1.2 add_log_fusion
  193.0 0.6 fusion.20
  193.6 0.5 broadcast_multiply_fusion.1
  (1 shorter events, 0.0 us)
Async XLA Ops:
  7.2 82.1 %all-gather.3.cloned.1.call-start = ((), (), s32[]{:S(2)}) async-start(), calls=%async_computation.1 | async-start | bytes 4423680 | tf_op jit(solution)/shard_map/all_gather | solution.py:50
  10.5 0.7 copy-start
  10.5 0.8 copy-start.1
  25.9 61.2 %all-to-all-start = ((bf16[2,2,4,8,3,1,73,24]{6,7,4,2,1,5,0,3:T(8,128)(2,1)}), bf16[2,2,4,8,3,1,73,24]{6,7,4,2,1,5,0,3:T(8,128)(2,1)S(1)}, u32[]{:S(2)}, u32[]{:S(2)}) async-start(bf16[2,2,4,8,3,1,73,24]{6,7,4,2,1,5,0,3:T(8,128)(2,1)} %copy.32), calls=%async_computation | async-start | bytes 4718592 | tf_op jit(solution)/shard_map/all_to_all | solution.py:46
  33.5 134.1 %all-reduce.2.cloned.1.call-start = ((), (), s32[]{:S(2)}) async-start(), calls=%async_computation.2 | async-start | bytes 897024 | tf_op jit(solution)/shard_map/psum | solution.py:57
  96.1 93.3 %all-gather.5.cloned.1.call-start = ((), (), s32[]{:S(2)}) async-start(), calls=%async_computation.3 | async-start | bytes 2242560 | tf_op jit(solution)/shard_map/all_gather | solution.py:58
Sparse Core Ops, SparseCore 0:
  9.5 33.4 all-gather.2
  96.2 71.2 all-reduce.1
  169.1 20.2 all-gather.4
